TPU v7x, 128 devices: a whole 4x4x4 slice. The times are simulated.
128 devices in a mesh: row: 8 (over z, y_hi), col: 16 (over x, y_lo, core).
Axes of the slice: x: 4, y: 4 (y_hi: 2, y_lo: 2; y = y_hi * 2 + y_lo), z: 4, core: 2. Of those that a mesh axis runs over, the one named last changes fastest.
Arguments:
- tri_panels: float32 [8192, 8192], P('row', 'col'), may hold values from -1 to 2, as said below
- rhs_rows: float32 [8192, 2048], P(('row', 'col')), may hold values from -6 to 6
Outputs:
- rhs_grid: float32 [8192, 2048], P('row', 'col')
Inputs may be any that keep to these rules, and one draw needn't show every extreme that they name: `tri_panels`: in L's row order the entries above the diagonal are zero and the diagonal entries are positive.
All inputs are finite; a program needn't handle non-finite values.
Results may differ from a plain program's by a relative error of at most 0.00011.
Values sent between devices are 32-bit elements; how exact they have to be, the bound alone decides.
A program may use at most 256 MiB of HBM per device.

v0:
```python
import jax
import jax.numpy as jnp
from jax import lax
from jax.sharding import PartitionSpec as P


def picked(array, axis, root):
    return lax.dynamic_index_in_dim(lax.all_gather(array, axis), root, 0, keepdims=False)


def on_device(tri_panels, rhs_rows):
    row_count = lax.axis_size("row")
    col_count = lax.axis_size("col")
    row_position = lax.axis_index("row")
    col_position = lax.axis_index("col")
    local_rows, block_size = tri_panels.shape
    blocks = local_rows // block_size
    sub_rows = block_size // col_count
    parted = rhs_rows.reshape(blocks, sub_rows, rhs_rows.shape[1])
    state_rhs = lax.all_to_all(parted, "col", split_axis=2, concat_axis=1, tiled=True)
    identity_block = jnp.eye(block_size, dtype=jnp.float32)
    own_pieces = tri_panels.reshape(blocks, block_size, block_size)
    own_diag = lax.dynamic_index_in_dim(own_pieces, col_position // row_count, 0, keepdims=False)
    own_diag = jnp.where(col_position % row_count == row_position, own_diag, identity_block)
    own_inverse = jax.scipy.linalg.solve_triangular(own_diag, identity_block, lower=True)

    def advance(state_rhs, panel_cols, inverse_block, step_index, first_slot):
        count = blocks - first_slot
        owner_row = step_index % row_count
        slot_index = step_index // row_count
        pieces = panel_cols.reshape(count, block_size, block_size)
        current = lax.dynamic_index_in_dim(state_rhs, slot_index, 0, keepdims=False)
        local_solution = jnp.dot(
            inverse_block,
            current,
            precision=lax.Precision.HIGHEST,
            preferred_element_type=jnp.float32,
        )
        solution = picked(local_solution, "row", owner_row)
        stored = jnp.where(row_position == owner_row, solution, current)
        state_rhs = lax.dynamic_update_index_in_dim(state_rhs, stored, slot_index, 0)
        global_block = (first_slot + jnp.arange(count, dtype=jnp.int32)) * row_count + row_position
        product = jnp.einsum("sij,jc->sic", pieces, solution, precision=lax.Precision.HIGHEST)
        trailing = state_rhs[first_slot:]
        trailing = jnp.where(
            (global_block > step_index)[:, None, None], trailing - product, trailing
        )
        if first_slot > 0:
            return jnp.concatenate([state_rhs[:first_slot], trailing], 0)
        return trailing

    group_count = (col_count + row_count - 1) // row_count
    everything, inverses = (
        lax.all_gather(tri_panels, "col", axis=1, tiled=True),
        lax.all_gather(own_inverse, "col", axis=1, tiled=True),
    )
    for first_slot in range(group_count):
        begin_step = first_slot * row_count
        end_step = min(begin_step + row_count, col_count)
        own_rows = everything[first_slot * block_size :]

        def upfront_step(step_index, state_rhs, own_rows=own_rows, first_slot=first_slot):
            panel_cols = lax.dynamic_slice_in_dim(own_rows, step_index * block_size, block_size, 1)
            inverse_block = lax.dynamic_slice_in_dim(
                inverses, step_index * block_size, block_size, 1
            )
            return advance(state_rhs, panel_cols, inverse_block, step_index, first_slot)

        state_rhs = lax.fori_loop(begin_step, end_step, upfront_step, state_rhs)
    return state_rhs.reshape(local_rows, state_rhs.shape[2])


def solution(mesh):
    return jax.shard_map(
        on_device,
        mesh=mesh,
        in_specs=(P("row", "col"), P(("row", "col"), None)),
        out_specs=P("row", "col"),
        check_vma=False,
    )
```

profile of v0, /device:TPU:0, one launch (start us, length us, event | category | flops | bytes accessed | tf_op | source)
XLA Modules:
  0.0 1225.2 jit_solution(3915089604845928567)
XLA Ops:
  9.3 11.6 while.33
  20.9 39.3 %custom-call.4 = f32[4,128,128]{1,2,0:T(8,128)S(1)} custom-call(f32[4,128,128]{2,1,0:T(8,128)S(1)} %get-tuple-element.290), custom_call_target="InvertDiagBlocksLowerTriangular" | custom-call | tf_op jit(solution)/shard_map/jit(_solve_triangular)/triangular_solve | solution.py:25
  76.7 14.4 %all-to-all-done = f32[16,1,8192]{2,1,0:T(1,128)S(1)} async-done(((f32[16,1,8192]{2,1,0:T(1,128)}), f32[16,1,8192]{2,1,0:T(1,128)S(1)}, u32[]{:S(2)}, u32[]{:S(2)}) %all-to-all-start) | async-done | bytes 524320 | tf_op jit(solution)/shard_map/all_to_all | solution.py:20
  96.2 91.5 %all-gather.13.cloned.1.call-done = f32[1024,8192]{1,0:T(8,128)} async-done(((f32[1024,512]{1,0:T(8,128)}), f32[1024,8192]{1,0:T(8,128)}) %all-gather.13.cloned.1.call-update) | async-done | bytes 33554448 | tf_op jit(solution)/shard_map/all_gather | solution.py:54
  187.7 11.5 slice.70
  199.2 82.4 %all-gather.11.cloned.1.call-done = f32[512,8192]{1,0:T(8,128)} async-done(((f32[512,512]{1,0:T(8,128)}), f32[512,8192]{1,0:T(8,128)}) %all-gather.11.cloned.1.call-update) | async-done | bytes 16777232 | tf_op jit(solution)/shard_map/all_gather | solution.py:55
  281.6 471.9 %while.31 = (s32[]{:T(128)}, f32[2,512,128]{2,1,0:T(8,128)S(1)}, s32[]{:T(128)}, f32[512,8192]{1,0:T(8,128)}, f32[1024,8192]{1,0:T(8,128)}, /*index=5*/s32[]{:T(...) while((s32[]{:T(128)}, f32[2,512,128]{2,1,0:T(8,128)S(1)}, ...), condition=%wide.region_1.2_spmd, body=%wide.region_0.1_spmd.sunk | while | flops 1208287232 | bytes 17039816 | solution.py:69
  286.3 53.0 %all-gather.15.cloned.1.call-done = f32[4096,128]{1,0:T(8,128)} async-done(((f32[512,128]{1,0:T(8,128)}), f32[4096,128]{1,0:T(8,128)}) %all-gather.15.cloned.1.call-update) | async-done | bytes 2097168 | tf_op jit(solution)/shard_map/while/body/eval_jaxpr/all_gather | solution.py:8
  348.1 49.8 %all-gather.15.cloned.1.call-done = f32[4096,128]{1,0:T(8,128)} async-done(((f32[512,128]{1,0:T(8,128)}), f32[4096,128]{1,0:T(8,128)}) %all-gather.15.cloned.1.call-update) | async-done | bytes 2097168 | tf_op jit(solution)/shard_map/while/body/eval_jaxpr/all_gather | solution.py:8
  406.7 49.8 %all-gather.15.cloned.1.call-done = f32[4096,128]{1,0:T(8,128)} async-done(((f32[512,128]{1,0:T(8,128)}), f32[4096,128]{1,0:T(8,128)}) %all-gather.15.cloned.1.call-update) | async-done | bytes 2097168 | tf_op jit(solution)/shard_map/while/body/eval_jaxpr/all_gather | solution.py:8
  465.3 49.8 %all-gather.15.cloned.1.call-done = f32[4096,128]{1,0:T(8,128)} async-done(((f32[512,128]{1,0:T(8,128)}), f32[4096,128]{1,0:T(8,128)}) %all-gather.15.cloned.1.call-update) | async-done | bytes 2097168 | tf_op jit(solution)/shard_map/while/body/eval_jaxpr/all_gather | solution.py:8
  523.9 49.8 %all-gather.15.cloned.1.call-done = f32[4096,128]{1,0:T(8,128)} async-done(((f32[512,128]{1,0:T(8,128)}), f32[4096,128]{1,0:T(8,128)}) %all-gather.15.cloned.1.call-update) | async-done | bytes 2097168 | tf_op jit(solution)/shard_map/while/body/eval_jaxpr/all_gather | solution.py:8
  582.5 49.8 %all-gather.15.cloned.1.call-done = f32[4096,128]{1,0:T(8,128)} async-done(((f32[512,128]{1,0:T(8,128)}), f32[4096,128]{1,0:T(8,128)}) %all-gather.15.cloned.1.call-update) | async-done | bytes 2097168 | tf_op jit(solution)/shard_map/while/body/eval_jaxpr/all_gather | solution.py:8
  641.1 49.8 %all-gather.15.cloned.1.call-done = f32[4096,128]{1,0:T(8,128)} async-done(((f32[512,128]{1,0:T(8,128)}), f32[4096,128]{1,0:T(8,128)}) %all-gather.15.cloned.1.call-update) | async-done | bytes 2097168 | tf_op jit(solution)/shard_map/while/body/eval_jaxpr/all_gather | solution.py:8
  699.8 49.8 %all-gather.15.cloned.1.call-done = f32[4096,128]{1,0:T(8,128)} async-done(((f32[512,128]{1,0:T(8,128)}), f32[4096,128]{1,0:T(8,128)}) %all-gather.15.cloned.1.call-update) | async-done | bytes 2097168 | tf_op jit(solution)/shard_map/while/body/eval_jaxpr/all_gather | solution.py:8
  753.5 464.0 %while.32 = (s32[]{:T(128)}, f32[2,512,128]{2,1,0:T(8,128)S(1)}, s32[]{:T(128)}, f32[512,8192]{1,0:T(8,128)}, s32[1]{0:T(128)}, /*index=5*/f32[512,8192]{1,0:T(8...) while((s32[]{:T(128)}, f32[2,512,128]{2,1,0:T(8,128)S(1)}, ...), condition=%wide.region_3.4_spmd, body=%wide.region_2.3_spmd.sunk | while | flops 805634048 | bytes 12846105 | solution.py:69
  756.6 51.6 %all-gather.17.cloned.1.call-done = f32[4096,128]{1,0:T(8,128)} async-done(((f32[512,128]{1,0:T(8,128)}), f32[4096,128]{1,0:T(8,128)}) %all-gather.17.cloned.1.call-update) | async-done | bytes 2097168 | tf_op jit(solution)/shard_map/while/body/eval_jaxpr/all_gather | solution.py:8
  814.6 51.6 %all-gather.17.cloned.1.call-done = f32[4096,128]{1,0:T(8,128)} async-done(((f32[512,128]{1,0:T(8,128)}), f32[4096,128]{1,0:T(8,128)}) %all-gather.17.cloned.1.call-update) | async-done | bytes 2097168 | tf_op jit(solution)/shard_map/while/body/eval_jaxpr/all_gather | solution.py:8
  872.6 51.6 %all-gather.17.cloned.1.call-done = f32[4096,128]{1,0:T(8,128)} async-done(((f32[512,128]{1,0:T(8,128)}), f32[4096,128]{1,0:T(8,128)}) %all-gather.17.cloned.1.call-update) | async-done | bytes 2097168 | tf_op jit(solution)/shard_map/while/body/eval_jaxpr/all_gather | solution.py:8
  930.6 51.6 %all-gather.17.cloned.1.call-done = f32[4096,128]{1,0:T(8,128)} async-done(((f32[512,128]{1,0:T(8,128)}), f32[4096,128]{1,0:T(8,128)}) %all-gather.17.cloned.1.call-update) | async-done | bytes 2097168 | tf_op jit(solution)/shard_map/while/body/eval_jaxpr/all_gather | solution.py:8
  988.6 51.6 %all-gather.17.cloned.1.call-done = f32[4096,128]{1,0:T(8,128)} async-done(((f32[512,128]{1,0:T(8,128)}), f32[4096,128]{1,0:T(8,128)}) %all-gather.17.cloned.1.call-update) | async-done | bytes 2097168 | tf_op jit(solution)/shard_map/while/body/eval_jaxpr/all_gather | solution.py:8
  1046.6 51.6 %all-gather.17.cloned.1.call-done = f32[4096,128]{1,0:T(8,128)} async-done(((f32[512,128]{1,0:T(8,128)}), f32[4096,128]{1,0:T(8,128)}) %all-gather.17.cloned.1.call-update) | async-done | bytes 2097168 | tf_op jit(solution)/shard_map/while/body/eval_jaxpr/all_gather | solution.py:8
  1104.6 51.6 %all-gather.17.cloned.1.call-done = f32[4096,128]{1,0:T(8,128)} async-done(((f32[512,128]{1,0:T(8,128)}), f32[4096,128]{1,0:T(8,128)}) %all-gather.17.cloned.1.call-update) | async-done | bytes 2097168 | tf_op jit(solution)/shard_map/while/body/eval_jaxpr/all_gather | solution.py:8
  1162.6 51.6 %all-gather.17.cloned.1.call-done = f32[4096,128]{1,0:T(8,128)} async-done(((f32[512,128]{1,0:T(8,128)}), f32[4096,128]{1,0:T(8,128)}) %all-gather.17.cloned.1.call-update) | async-done | bytes 2097168 | tf_op jit(solution)/shard_map/while/body/eval_jaxpr/all_gather | solution.py:8
  (155 shorter events, 156.3 us)
Async XLA Ops:
  6.5 1.6 copy-start.1
  6.5 181.1 %all-gather.13.cloned.1.call-start = ((), (), s32[]{:S(2)}) async-start(), calls=%async_computation.2 | async-start | bytes 35651584 | tf_op jit(solution)/shard_map/all_gather | solution.py:54
  7.3 274.3 %all-gather.11.cloned.1.call-start = ((), (), s32[]{:S(2)}) async-start(), calls=%async_computation.1 | async-start | bytes 17825792 | tf_op jit(solution)/shard_map/all_gather | solution.py:55
  65.7 1.5 copy-start.2
  71.1 20.0 %all-to-all-start = ((f32[16,1,8192]{2,1,0:T(1,128)}), f32[16,1,8192]{2,1,0:T(1,128)S(1)}, u32[]{:S(2)}, u32[]{:S(2)}) async-start(f32[16,1,8192]{2,1,0:T(1,128)} %reshape.83), calls=%async_computation | async-start | bytes 1048576 | tf_op jit(solution)/shard_map/all_to_all | solution.py:20
  281.6 57.7 %all-gather.15.cloned.1.call-start = ((), (), s32[]{:S(2)}) async-start(), calls=%async_computation.3 | async-start | bytes 2359296 | tf_op jit(solution)/shard_map/while/body/eval_jaxpr/all_gather | solution.py:8
  343.3 54.6 %all-gather.15.cloned.1.call-start = ((), (), s32[]{:S(2)}) async-start(), calls=%async_computation.3 | async-start | bytes 2359296 | tf_op jit(solution)/shard_map/while/body/eval_jaxpr/all_gather | solution.py:8
  401.9 54.6 %all-gather.15.cloned.1.call-start = ((), (), s32[]{:S(2)}) async-start(), calls=%async_computation.3 | async-start | bytes 2359296 | tf_op jit(solution)/shard_map/while/body/eval_jaxpr/all_gather | solution.py:8
  460.5 54.6 %all-gather.15.cloned.1.call-start = ((), (), s32[]{:S(2)}) async-start(), calls=%async_computation.3 | async-start | bytes 2359296 | tf_op jit(solution)/shard_map/while/body/eval_jaxpr/all_gather | solution.py:8
  519.1 54.7 %all-gather.15.cloned.1.call-start = ((), (), s32[]{:S(2)}) async-start(), calls=%async_computation.3 | async-start | bytes 2359296 | tf_op jit(solution)/shard_map/while/body/eval_jaxpr/all_gather | solution.py:8
  577.7 54.6 %all-gather.15.cloned.1.call-start = ((), (), s32[]{:S(2)}) async-start(), calls=%async_computation.3 | async-start | bytes 2359296 | tf_op jit(solution)/shard_map/while/body/eval_jaxpr/all_gather | solution.py:8
  636.3 54.6 %all-gather.15.cloned.1.call-start = ((), (), s32[]{:S(2)}) async-start(), calls=%async_computation.3 | async-start | bytes 2359296 | tf_op jit(solution)/shard_map/while/body/eval_jaxpr/all_gather | solution.py:8
  694.9 54.6 %all-gather.15.cloned.1.call-start = ((), (), s32[]{:S(2)}) async-start(), calls=%async_computation.3 | async-start | bytes 2359296 | tf_op jit(solution)/shard_map/while/body/eval_jaxpr/all_gather | solution.py:8
  753.6 54.6 %all-gather.17.cloned.1.call-start = ((), (), s32[]{:S(2)}) async-start(), calls=%async_computation.4 | async-start | bytes 2359296 | tf_op jit(solution)/shard_map/while/body/eval_jaxpr/all_gather | solution.py:8
  811.6 54.6 %all-gather.17.cloned.1.call-start = ((), (), s32[]{:S(2)}) async-start(), calls=%async_computation.4 | async-start | bytes 2359296 | tf_op jit(solution)/shard_map/while/body/eval_jaxpr/all_gather | solution.py:8
  869.5 54.7 %all-gather.17.cloned.1.call-start = ((), (), s32[]{:S(2)}) async-start(), calls=%async_computation.4 | async-start | bytes 2359296 | tf_op jit(solution)/shard_map/while/body/eval_jaxpr/all_gather | solution.py:8
  927.6 54.6 %all-gather.17.cloned.1.call-start = ((), (), s32[]{:S(2)}) async-start(), calls=%async_computation.4 | async-start | bytes 2359296 | tf_op jit(solution)/shard_map/while/body/eval_jaxpr/all_gather | solution.py:8
  985.5 54.6 %all-gather.17.cloned.1.call-start = ((), (), s32[]{:S(2)}) async-start(), calls=%async_computation.4 | async-start | bytes 2359296 | tf_op jit(solution)/shard_map/while/body/eval_jaxpr/all_gather | solution.py:8
  1043.5 54.6 %all-gather.17.cloned.1.call-start = ((), (), s32[]{:S(2)}) async-start(), calls=%async_computation.4 | async-start | bytes 2359296 | tf_op jit(solution)/shard_map/while/body/eval_jaxpr/all_gather | solution.py:8
  1101.5 54.6 %all-gather.17.cloned.1.call-start = ((), (), s32[]{:S(2)}) async-start(), calls=%async_computation.4 | async-start | bytes 2359296 | tf_op jit(solution)/shard_map/while/body/eval_jaxpr/all_gather | solution.py:8
  1159.5 54.6 %all-gather.17.cloned.1.call-start = ((), (), s32[]{:S(2)}) async-start(), calls=%async_computation.4 | async-start | bytes 2359296 | tf_op jit(solution)/shard_map/while/body/eval_jaxpr/all_gather | solution.py:8
  1217.5 0.8 copy-start
Sparse Core Ops, SparseCore 0:
  9.0 178.6 all-gather.12
  189.3 92.2 all-gather.10
  284.7 54.5 all-gather.14
  346.4 51.4 all-gather.14
  405.0 51.4 all-gather.14
  463.6 51.4 all-gather.14
  522.2 51.4 all-gather.14
  580.9 51.4 all-gather.14
  639.5 51.4 all-gather.14
  698.1 51.4 all-gather.14
  756.7 51.4 all-gather.16
  814.7 51.4 all-gather.16
  872.7 51.4 all-gather.16
  930.7 51.4 all-gather.16
  988.7 51.4 all-gather.16
  1046.7 51.4 all-gather.16
  1104.7 51.4 all-gather.16
  1162.7 51.4 all-gather.16
where the time goes:
time: 1230 us
  waiting for transfers between devices  1000 us (81%)
  matrix products  94.2 us (8%)
  other arithmetic  59.8 us (5%)
  local copies, waits for them, and re-layouts  45.9 us (4%)
  between operations  13.6 us (1%)
    all_gather x16, waiting for transfers between devices, picked(): lax.all_gather(array, axis)  814 us
    all_gather x1, waiting for transfers between devices, on_device(): lax.all_gather(tri_panels, 'col', axis=1, tiled=True)  91.5 us
    all_gather x1, waiting for transfers between devices, on_device(): lax.all_gather(own_inverse, 'col', axis=1, tiled=True)  82.4 us
    dot_general x16, matrix products, advance(): jnp.dot(inverse_block, current, precision=lax.Precision.HIGHEST, preferre...  46.7 us
    dot_general x16, matrix products, advance(): jnp.einsum('sij,jc->sic', pieces, solution, precision=lax.Precision.HIGHEST)  41.8 us
    another operation x4, other arithmetic, on_device(): jax.scipy.linalg.solve_triangular(own_diag, identity_block, lower=True)  41.5 us
  transfers between devices with their start and end apart: 19, of which 19 were waited for; matrix products, arithmetic and copies ran while one was open for 8% of the time, Pallas kernels for 0%

commit v1 on v0

--- a/solution.py
+++ b/solution.py
@@ -51,7 +51,9 @@
 
     group_count = (col_count + row_count - 1) // row_count
     everything, inverses = (
-        lax.all_gather(tri_panels, "col", axis=1, tiled=True),
+        jnp.concatenate(
+            lax.all_to_all(jnp.stack([tri_panels] * lax.axis_size("col")), "col", 0, 0), axis=1
+        ),
         lax.all_gather(own_inverse, "col", axis=1, tiled=True),
     )
     for first_slot in range(group_count):

time: 1230 us -> 1620 us (1.32)
  waiting for transfers between devices: 1000 us -> 1300 us
  local copies, waits for them, and re-layouts: 45.9 us -> 121 us
    all_to_all x0 -> x1, waiting for transfers between devices: none -> 484 us  [on_device(): lax.all_to_all(jnp.stack([tri_panels] * lax.axis_size('col')), 'col', 0, 0)]
    all_gather x1 -> x0, waiting for transfers between devices: 91.5 us -> none  [on_device(): lax.all_gather(tri_panels, 'col', axis=1, tiled=True)]
    all_gather x1, waiting for transfers between devices: 82.4 us -> 0.01 us  [on_device(): lax.all_gather(own_inverse, 'col', axis=1, tiled=True)]
    all_to_all x0 -> x1, local copies, waits for them, and re-layouts: none -> 31.8 us  [on_device(): lax.all_to_all(jnp.stack([tri_panels] * lax.axis_size('col')), 'col', 0, 0)]
    dynamic_slice x8 -> x16, local copies, waits for them, and re-layouts: 14.2 us -> 41.3 us  [upfront_step(): lax.dynamic_slice_in_dim(own_rows, step_index * block_size, block_size, 1)]
  transfers between devices with their start and end apart: 19 -> 19, of which waited for: 19 -> 17; matrix products, arithmetic and copies ran while one was open for 8% -> 10% of each run, Pallas kernels for 0% -> 0%
where the time goes in v1:
time: 1620 us; the launch traced here: 1610 us
  waiting for transfers between devices  1300 us (80%)
  local copies, waits for them, and re-layouts  121 us (7%)
  matrix products  103 us (6%)
  other arithmetic  61.6 us (4%)
    all_gather x16, waiting for transfers between devices, picked(): lax.all_gather(array, axis)  818 us
    all_to_all x1, waiting for transfers between devices, on_device(): lax.all_to_all(jnp.stack([tri_panels] * lax.axis_size('col')), 'col', 0, 0)  484 us
    dot_general x16, matrix products, advance(): jnp.einsum('sij,jc->sic', pieces, solution, precision=lax.Precision.HIGHEST)  48.3 us
    dot_general x16, matrix products, advance(): jnp.dot(inverse_block, current, precision=lax.Precision.HIGHEST, preferre...  46.7 us
    another operation x4, other arithmetic, on_device(): jax.scipy.linalg.solve_triangular(own_diag, identity_block, lower=True)  42.3 us
    dynamic_slice x16, local copies, waits for them, and re-layouts, upfront_step(): lax.dynamic_slice_in_dim(own_rows, step_index * block_size, block_size, 1)  41.3 us
  transfers between devices with their start and end apart: 19, of which 17 were waited for; matrix products, arithmetic and copies ran while one was open for 10% of the time, Pallas kernels for 0%

profile of v1, /device:TPU:0, one launch (start us, length us, event | category | flops | bytes accessed | tf_op | source)
XLA Modules:
  0.0 1614.6 jit_solution(6475875258240399321)
XLA Ops:
  19.9 14.4 while.33
  34.3 40.1 %custom-call.4 = f32[4,128,128]{1,2,0:T(8,128)S(1)} custom-call(f32[4,128,128]{2,1,0:T(8,128)} %get-tuple-element.290), custom_call_target="InvertDiagBlocksLowerTriangular" | custom-call | tf_op jit(solution)/shard_map/jit(_solve_triangular)/triangular_solve | solution.py:25
  82.9 11.3 stack.2
  106.6 483.9 %all-to-all-done.1 = f32[16,1024,512]{2,1,0:T(8,128)} async-done(((f32[16,1024,512]{2,1,0:T(8,128)}), f32[16,1024,512]{2,1,0:T(8,128)}, u32[]{:S(2)}, u32[]{:S(2)}) %all-to-all-start.1) | async-done | bytes 33554464 | tf_op jit(solution)/shard_map/all_to_all | solution.py:55
  590.5 31.8 %copy.10 = f32[16,1024,512]{1,2,0:T(8,128)} copy(f32[16,1024,512]{2,1,0:T(8,128)} %all-to-all-done.1) | data formatting | bytes 67108864 | tf_op jit(solution)/shard_map/all_to_all | solution.py:55
  622.3 11.6 slice.74
  633.9 502.8 %while.31 = (s32[]{:T(128)}, f32[2,512,128]{2,1,0:T(8,128)S(1)}, s32[]{:T(128)}, f32[512,8192]{1,0:T(8,128)}, f32[1024,8192]{0,1:T(8,128)}, /*index=5*/s32[]{:T(...) while((s32[]{:T(128)}, f32[2,512,128]{2,1,0:T(8,128)S(1)}, ...), condition=%wide.region_1.2_spmd, body=%wide.region_0.1_spmd.sunk | while | flops 1208287232 | bytes 21234120 | solution.py:71
  642.0 80.4 %all-gather.12.cloned.1.call-done = f32[4096,128]{1,0:T(8,128)} async-done(((f32[512,128]{1,0:T(8,128)}), f32[4096,128]{1,0:T(8,128)}) %all-gather.12.cloned.1.call-update) | async-done | bytes 2097168 | tf_op jit(solution)/shard_map/while/body/eval_jaxpr/all_gather | solution.py:8
  734.7 46.4 %all-gather.12.cloned.1.call-done = f32[4096,128]{1,0:T(8,128)} async-done(((f32[512,128]{1,0:T(8,128)}), f32[4096,128]{1,0:T(8,128)}) %all-gather.12.cloned.1.call-update) | async-done | bytes 2097168 | tf_op jit(solution)/shard_map/while/body/eval_jaxpr/all_gather | solution.py:8
  793.3 46.4 %all-gather.12.cloned.1.call-done = f32[4096,128]{1,0:T(8,128)} async-done(((f32[512,128]{1,0:T(8,128)}), f32[4096,128]{1,0:T(8,128)}) %all-gather.12.cloned.1.call-update) | async-done | bytes 2097168 | tf_op jit(solution)/shard_map/while/body/eval_jaxpr/all_gather | solution.py:8
  851.9 46.4 %all-gather.12.cloned.1.call-done = f32[4096,128]{1,0:T(8,128)} async-done(((f32[512,128]{1,0:T(8,128)}), f32[4096,128]{1,0:T(8,128)}) %all-gather.12.cloned.1.call-update) | async-done | bytes 2097168 | tf_op jit(solution)/shard_map/while/body/eval_jaxpr/all_gather | solution.py:8
  910.5 46.4 %all-gather.12.cloned.1.call-done = f32[4096,128]{1,0:T(8,128)} async-done(((f32[512,128]{1,0:T(8,128)}), f32[4096,128]{1,0:T(8,128)}) %all-gather.12.cloned.1.call-update) | async-done | bytes 2097168 | tf_op jit(solution)/shard_map/while/body/eval_jaxpr/all_gather | solution.py:8
  969.1 46.4 %all-gather.12.cloned.1.call-done = f32[4096,128]{1,0:T(8,128)} async-done(((f32[512,128]{1,0:T(8,128)}), f32[4096,128]{1,0:T(8,128)}) %all-gather.12.cloned.1.call-update) | async-done | bytes 2097168 | tf_op jit(solution)/shard_map/while/body/eval_jaxpr/all_gather | solution.py:8
  1027.7 46.4 %all-gather.12.cloned.1.call-done = f32[4096,128]{1,0:T(8,128)} async-done(((f32[512,128]{1,0:T(8,128)}), f32[4096,128]{1,0:T(8,128)}) %all-gather.12.cloned.1.call-update) | async-done | bytes 2097168 | tf_op jit(solution)/shard_map/while/body/eval_jaxpr/all_gather | solution.py:8
  1086.3 46.4 %all-gather.12.cloned.1.call-done = f32[4096,128]{1,0:T(8,128)} async-done(((f32[512,128]{1,0:T(8,128)}), f32[4096,128]{1,0:T(8,128)}) %all-gather.12.cloned.1.call-update) | async-done | bytes 2097168 | tf_op jit(solution)/shard_map/while/body/eval_jaxpr/all_gather | solution.py:8
  1136.7 470.5 %while.32 = (s32[]{:T(128)}, f32[2,512,128]{2,1,0:T(8,128)S(1)}, s32[]{:T(128)}, f32[512,8192]{1,0:T(8,128)}, s32[1]{0:T(128)}, /*index=5*/f32[512,8192]{0,1:T(8...) while((s32[]{:T(128)}, f32[2,512,128]{2,1,0:T(8,128)S(1)}, ...), condition=%wide.region_3.4_spmd, body=%wide.region_2.3_spmd.sunk | while | flops 805634048 | bytes 12846105 | solution.py:71
  1139.8 51.6 %all-gather.14.cloned.1.call-done = f32[4096,128]{1,0:T(8,128)} async-done(((f32[512,128]{1,0:T(8,128)}), f32[4096,128]{1,0:T(8,128)}) %all-gather.14.cloned.1.call-update) | async-done | bytes 2097168 | tf_op jit(solution)/shard_map/while/body/eval_jaxpr/all_gather | solution.py:8
  1198.6 51.6 %all-gather.14.cloned.1.call-done = f32[4096,128]{1,0:T(8,128)} async-done(((f32[512,128]{1,0:T(8,128)}), f32[4096,128]{1,0:T(8,128)}) %all-gather.14.cloned.1.call-update) | async-done | bytes 2097168 | tf_op jit(solution)/shard_map/while/body/eval_jaxpr/all_gather | solution.py:8
  1257.5 51.6 %all-gather.14.cloned.1.call-done = f32[4096,128]{1,0:T(8,128)} async-done(((f32[512,128]{1,0:T(8,128)}), f32[4096,128]{1,0:T(8,128)}) %all-gather.14.cloned.1.call-update) | async-done | bytes 2097168 | tf_op jit(solution)/shard_map/while/body/eval_jaxpr/all_gather | solution.py:8
  1316.3 51.6 %all-gather.14.cloned.1.call-done = f32[4096,128]{1,0:T(8,128)} async-done(((f32[512,128]{1,0:T(8,128)}), f32[4096,128]{1,0:T(8,128)}) %all-gather.14.cloned.1.call-update) | async-done | bytes 2097168 | tf_op jit(solution)/shard_map/while/body/eval_jaxpr/all_gather | solution.py:8
  1375.1 51.6 %all-gather.14.cloned.1.call-done = f32[4096,128]{1,0:T(8,128)} async-done(((f32[512,128]{1,0:T(8,128)}), f32[4096,128]{1,0:T(8,128)}) %all-gather.14.cloned.1.call-update) | async-done | bytes 2097168 | tf_op jit(solution)/shard_map/while/body/eval_jaxpr/all_gather | solution.py:8
  1433.9 51.6 %all-gather.14.cloned.1.call-done = f32[4096,128]{1,0:T(8,128)} async-done(((f32[512,128]{1,0:T(8,128)}), f32[4096,128]{1,0:T(8,128)}) %all-gather.14.cloned.1.call-update) | async-done | bytes 2097168 | tf_op jit(solution)/shard_map/while/body/eval_jaxpr/all_gather | solution.py:8
  1492.7 51.6 %all-gather.14.cloned.1.call-done = f32[4096,128]{1,0:T(8,128)} async-done(((f32[512,128]{1,0:T(8,128)}), f32[4096,128]{1,0:T(8,128)}) %all-gather.14.cloned.1.call-update) | async-done | bytes 2097168 | tf_op jit(solution)/shard_map/while/body/eval_jaxpr/all_gather | solution.py:8
  1551.5 51.6 %all-gather.14.cloned.1.call-done = f32[4096,128]{1,0:T(8,128)} async-done(((f32[512,128]{1,0:T(8,128)}), f32[4096,128]{1,0:T(8,128)}) %all-gather.14.cloned.1.call-update) | async-done | bytes 2097168 | tf_op jit(solution)/shard_map/while/body/eval_jaxpr/all_gather | solution.py:8
  (168 shorter events, 202.9 us)
Async XLA Ops:
  11.9 6.9 copy-start.1
  11.9 71.0 %all-to-all-start = ((f32[16,1,8192]{2,1,0:T(1,128)}), f32[16,1,8192]{2,1,0:T(1,128)S(1)}, u32[]{:S(2)}, u32[]{:S(2)}) async-start(f32[16,1,8192]{2,1,0:T(1,128)} %reshape.94), calls=%async_computation | async-start | bytes 1048576 | tf_op jit(solution)/shard_map/all_to_all | solution.py:20
  74.5 0.7 copy-start.3
  75.5 4.1 copy-start.4
  94.2 6.3 copy-start.2
  94.2 496.3 %all-to-all-start.1 = ((f32[16,1024,512]{2,1,0:T(8,128)}), f32[16,1024,512]{2,1,0:T(8,128)}, u32[]{:S(2)}, u32[]{:S(2)}) async-start(f32[16,1024,512]{2,1,0:T(8,128)} %stack.2), calls=%async_computation.1 | async-start | bytes 67108864 | tf_op jit(solution)/shard_map/all_to_all | solution.py:55
  100.3 533.6 %all-gather.10.cloned.1.call-start = ((), (), s32[]{:S(2)}) async-start(), calls=%async_computation.2 | async-start | bytes 17825792 | tf_op jit(solution)/shard_map/all_gather | solution.py:57
  633.9 88.6 %all-gather.12.cloned.1.call-start = ((), (), s32[]{:S(2)}) async-start(), calls=%async_computation.3 | async-start | bytes 2359296 | tf_op jit(solution)/shard_map/while/body/eval_jaxpr/all_gather | solution.py:8
  726.5 54.6 %all-gather.12.cloned.1.call-start = ((), (), s32[]{:S(2)}) async-start(), calls=%async_computation.3 | async-start | bytes 2359296 | tf_op jit(solution)/shard_map/while/body/eval_jaxpr/all_gather | solution.py:8
  785.1 54.6 %all-gather.12.cloned.1.call-start = ((), (), s32[]{:S(2)}) async-start(), calls=%async_computation.3 | async-start | bytes 2359296 | tf_op jit(solution)/shard_map/while/body/eval_jaxpr/all_gather | solution.py:8
  843.7 54.6 %all-gather.12.cloned.1.call-start = ((), (), s32[]{:S(2)}) async-start(), calls=%async_computation.3 | async-start | bytes 2359296 | tf_op jit(solution)/shard_map/while/body/eval_jaxpr/all_gather | solution.py:8
  902.3 54.6 %all-gather.12.cloned.1.call-start = ((), (), s32[]{:S(2)}) async-start(), calls=%async_computation.3 | async-start | bytes 2359296 | tf_op jit(solution)/shard_map/while/body/eval_jaxpr/all_gather | solution.py:8
  960.9 54.7 %all-gather.12.cloned.1.call-start = ((), (), s32[]{:S(2)}) async-start(), calls=%async_computation.3 | async-start | bytes 2359296 | tf_op jit(solution)/shard_map/while/body/eval_jaxpr/all_gather | solution.py:8
  1019.5 54.6 %all-gather.12.cloned.1.call-start = ((), (), s32[]{:S(2)}) async-start(), calls=%async_computation.3 | async-start | bytes 2359296 | tf_op jit(solution)/shard_map/while/body/eval_jaxpr/all_gather | solution.py:8
  1078.1 54.6 %all-gather.12.cloned.1.call-start = ((), (), s32[]{:S(2)}) async-start(), calls=%async_computation.3 | async-start | bytes 2359296 | tf_op jit(solution)/shard_map/while/body/eval_jaxpr/all_gather | solution.py:8
  1136.8 54.6 %all-gather.14.cloned.1.call-start = ((), (), s32[]{:S(2)}) async-start(), calls=%async_computation.4 | async-start | bytes 2359296 | tf_op jit(solution)/shard_map/while/body/eval_jaxpr/all_gather | solution.py:8
  1195.6 54.6 %all-gather.14.cloned.1.call-start = ((), (), s32[]{:S(2)}) async-start(), calls=%async_computation.4 | async-start | bytes 2359296 | tf_op jit(solution)/shard_map/while/body/eval_jaxpr/all_gather | solution.py:8
  1254.4 54.6 %all-gather.14.cloned.1.call-start = ((), (), s32[]{:S(2)}) async-start(), calls=%async_computation.4 | async-start | bytes 2359296 | tf_op jit(solution)/shard_map/while/body/eval_jaxpr/all_gather | solution.py:8
  1313.2 54.7 %all-gather.14.cloned.1.call-start = ((), (), s32[]{:S(2)}) async-start(), calls=%async_computation.4 | async-start | bytes 2359296 | tf_op jit(solution)/shard_map/while/body/eval_jaxpr/all_gather | solution.py:8
  1372.0 54.6 %all-gather.14.cloned.1.call-start = ((), (), s32[]{:S(2)}) async-start(), calls=%async_computation.4 | async-start | bytes 2359296 | tf_op jit(solution)/shard_map/while/body/eval_jaxpr/all_gather | solution.py:8
  1430.8 54.6 %all-gather.14.cloned.1.call-start = ((), (), s32[]{:S(2)}) async-start(), calls=%async_computation.4 | async-start | bytes 2359296 | tf_op jit(solution)/shard_map/while/body/eval_jaxpr/all_gather | solution.py:8
  1489.7 54.6 %all-gather.14.cloned.1.call-start = ((), (), s32[]{:S(2)}) async-start(), calls=%async_computation.4 | async-start | bytes 2359296 | tf_op jit(solution)/shard_map/while/body/eval_jaxpr/all_gather | solution.py:8
  1548.5 54.6 %all-gather.14.cloned.1.call-start = ((), (), s32[]{:S(2)}) async-start(), calls=%async_computation.4 | async-start | bytes 2359296 | tf_op jit(solution)/shard_map/while/body/eval_jaxpr/all_gather | solution.py:8
  1607.3 0.8 copy-start
Sparse Core Ops, SparseCore 0:
  102.7 440.4 all-gather.9
  637.1 85.3 all-gather.11
  729.6 51.4 all-gather.11
  788.2 51.4 all-gather.11
  846.8 51.4 all-gather.11
  905.4 51.4 all-gather.11
  964.0 51.4 all-gather.11
  1022.7 51.4 all-gather.11
  1081.3 51.4 all-gather.11
  1139.9 51.4 all-gather.13
  1198.7 51.4 all-gather.13
  1257.6 51.4 all-gather.13
  1316.4 51.4 all-gather.13
  1375.2 51.4 all-gather.13
  1434.0 51.4 all-gather.13
  1492.8 51.4 all-gather.13
  1551.6 51.4 all-gather.13
